TPU v7x, 256 devices: a whole 4x4x8 slice. The times are simulated.
256 devices in a mesh: front: 32 (over z, x), panel: 8 (over y, core).
Axes of the slice: x: 4, y: 4, z: 8, core: 2. Of those that a mesh axis runs over, the one named last changes fastest.
Arguments:
- coupling: bfloat16 [32, 2048, 2048], P('front', 'panel'), may hold values from -1 to 1
- pivot_inverse: bfloat16 [32, 2048, 2048], P('front', 'panel'), may hold values from -0.125 to 0.125
- pivots: float32 [32, 2048], P('front'), as said below
- trailing: float32 [32, 2048, 2048], P('front', 'panel'), may hold values from -12 to 12
- sketch: float32 [32, 8, 8, 32, 256], P('front', 'panel'), may hold values from -6 to 6
- extend_map: int32 [32, 2048], replicated, may hold values from 0 to 511, as said below
- parent_of: int32 [32], replicated, may hold values from 0 to 31, as said below
- parent_base: bfloat16 [32, 4096, 4096], P('front', 'panel'), may hold values from -6 to 6
Outputs:
- assembled: bfloat16 [32, 4096, 4096], P('front', 'panel')
Inputs may be any that keep to these rules, and one draw needn't show every extreme that they name: `extend_map`: within each front and each aligned block of 2048 / 8 entries the values are distinct and rising. `pivots`: every entry's magnitude lies between 0.5 and 2 times 2048 ** -0.5; signs are mixed. `parent_of`: no parent has more than 4 children; some parent has exactly 4.
All inputs are finite; a program needn't handle non-finite values.
Results may differ from a plain program's by a relative error of at most 0.0043.
Values may be sent and summed in bfloat16 or wider, within the bound.
A program may use at most 128 MiB of HBM per device.

v0:
```python
import jax
import jax.numpy as jnp
from jax import lax
from jax.sharding import PartitionSpec as P

MAXKIDS = 4


def compress_rows(schur, omega, tile_rows, tile_cols, tile_size):
    tiles = schur.reshape(tile_rows, tile_size, tile_cols, tile_size)
    range_t = jnp.einsum("ijkb,iajb->ijka", omega, tiles, precision=lax.Precision.HIGHEST)
    gram = jnp.einsum("ijka,ijla->ijkl", range_t, range_t, precision=lax.Precision.HIGHEST)
    lower = jnp.linalg.cholesky(gram)
    basis = jax.scipy.linalg.solve_triangular(lower, range_t, lower=True)
    coeff = jnp.einsum("ijka,iajb->ijkb", basis, tiles, precision=lax.Precision.HIGHEST)
    return (basis.astype(jnp.bfloat16), coeff.astype(jnp.bfloat16))


def body(coupling, pivot_inverse, pivots, trailing, sketch, extend_map, parent_of, parent_base):
    rows_here = coupling[0]
    row_dev = rows_here.shape[0]
    factor_sum = jnp.dot(
        rows_here,
        lax.all_gather(pivot_inverse, "panel", axis=1, tiled=True)[0],
        preferred_element_type=jnp.float32,
    )
    factor = factor_sum.astype(jnp.bfloat16)
    scaled = (factor.astype(jnp.float32) / pivots[0][None, :]).astype(jnp.bfloat16)
    gathered = lax.all_gather(factor, "panel", axis=0, tiled=True)
    update = lax.dot_general(
        scaled, gathered, (((1,), (1,)), ((), ())), preferred_element_type=jnp.float32
    )
    schur = trailing[0] - update
    omega = sketch[0]
    tile_rows = omega.shape[0]
    tile_cols = omega.shape[1]
    tile_size = omega.shape[3]
    basis, coeff = compress_rows(schur, omega, tile_rows, tile_cols, tile_size)
    contrib = tile_cols * tile_size
    parent_dev = parent_base.shape[1]
    parent_width = parent_base.shape[2]
    panels = lax.axis_size("panel")
    owner = lax.axis_index("front")
    panel_here = lax.axis_index("panel")
    targets = jnp.arange(parent_dev, dtype=jnp.int32)
    sources = jnp.arange(row_dev, dtype=jnp.int32)
    offsets = jnp.arange(panels, dtype=jnp.int32) * row_dev
    empty = jnp.zeros((parent_dev, parent_width), jnp.float32)

    def place(total, child, basis_f, coeff_f):
        maps = extend_map[child]
        row_map = lax.dynamic_slice_in_dim(maps, panel_here * row_dev, row_dev, 0)
        match_rows = row_map[None, :] == targets[:, None]
        source_rows = jnp.sum(jnp.where(match_rows, sources[None, :], 0), axis=1)
        valid_rows = jnp.any(match_rows, axis=1)
        blocks = maps.reshape(panels, row_dev)
        match_cols = blocks[:, None, :] == targets[None, :, None]
        source_cols = (
            jnp.sum(jnp.where(match_cols, sources[None, None, :], 0), axis=2) + offsets[:, None]
        ).reshape(parent_width)
        valid_cols = jnp.any(match_cols, axis=2).reshape(parent_width)
        dense = jnp.einsum(
            "ijka,ijkb->iajb", basis_f, coeff_f, preferred_element_type=jnp.float32
        ).reshape(row_dev, contrib)
        picked = jnp.take(jnp.take(dense, source_rows, axis=0), source_cols, axis=1)
        return total + jnp.where(valid_rows[:, None] & valid_cols[None, :], picked, 0.0)

    fronts = parent_of.shape[0]
    front_ids = jnp.arange(fronts, dtype=jnp.int32)
    same_parent = parent_of[:, None] == parent_of[None, :]
    position = jnp.sum(
        jnp.where(same_parent & (front_ids[None, :] < front_ids[:, None]), 1, 0), axis=1
    ).astype(jnp.int32)
    slot_ids = jnp.arange(MAXKIDS, dtype=jnp.int32)
    matches = (parent_of[None, :, None] == front_ids[:, None, None]) & (
        position[None, :, None] == slot_ids[None, None, :]
    )
    children = jnp.sum(jnp.where(matches, front_ids[None, :, None], 0), axis=1)
    present = jnp.any(matches, axis=1)
    packed = jnp.stack((basis, coeff)).reshape(fronts, -1)
    spread = lax.all_to_all(packed, "front", split_axis=0, concat_axis=0, tiled=True)
    chosen = jnp.take(spread, children.reshape(-1), axis=0)
    outgoing = jnp.where(present.reshape(-1)[:, None], chosen, jnp.zeros((), jnp.bfloat16)).reshape(
        fronts, MAXKIDS, -1
    )
    received = lax.all_to_all(outgoing, "front", split_axis=0, concat_axis=2, tiled=True)
    kids_data = received[0].reshape((MAXKIDS, 2) + basis.shape)
    mine = present[owner]
    kid_ids = children[owner]

    def one_slot(item, acc):
        return lax.cond(
            mine[item],
            lambda inner: place(inner, kid_ids[item], kids_data[item, 0], kids_data[item, 1]),
            lambda inner: inner,
            acc,
        )

    gathered_sum = lax.fori_loop(0, MAXKIDS, one_slot, empty)
    assembled = (parent_base[0].astype(jnp.float32) + gathered_sum).astype(jnp.bfloat16)
    return assembled[None]


def solution(mesh):
    placed = (
        P("front", "panel", None),
        P("front", "panel", None),
        P("front", None),
        P("front", "panel", None),
        P("front", "panel", None, None, None),
        P(),
        P(),
        P("front", "panel", None),
    )
    return jax.shard_map(
        body, mesh=mesh, in_specs=placed, out_specs=P("front", "panel", None), check_vma=False
    )
```

profile of v0, /device:TPU:66, one launch (start us, length us, event | category | flops | bytes accessed | tf_op | source)
XLA Modules:
  0.0 490.0 jit_solution(11895995338993416951)
XLA Ops:
  7.3 56.4 %all-gather.3.cloned.1.call-done = bf16[1,2048,2048]{2,1,0:T(8,128)(2,1)} async-done(((bf16[1,256,2048]{2,1,0:T(8,128)(2,1)}), bf16[1,2048,2048]{2,1,0:T(8,128)(2,1)}) %all-gather.3.cloned.1.call-update) | async-done | bytes 8388624 | tf_op jit(solution)/shard_map/all_gather | solution.py:24
  63.7 6.7 %fusion.20 = bf16[256,2048]{1,0:T(8,128)(2,1)} fusion(bf16[1,2048,2048]{2,1,0:T(8,128)(2,1)} %all-gather.3.cloned.1.call-done, bf16[1,256,2048]{2,1,0:T(8,128)(2,1)S(1)} %copy-done), kind=kOutput, calls=%fused_computation.40 | convolution fusion | flops 2148007936 | bytes 10485760 | tf_op jit(solution)/shard_map/dot_general | solution.py:22
  70.8 52.2 %all-gather.5.cloned.1.call-done = bf16[2048,2048]{1,0:T(8,128)(2,1)} async-done(((bf16[256,2048]{1,0:T(8,128)(2,1)}), bf16[2048,2048]{1,0:T(8,128)(2,1)}) %all-gather.5.cloned.1.call-update) | async-done | bytes 8388624 | tf_op jit(solution)/shard_map/all_gather | solution.py:29
  123.0 6.7 %convolution_subtract_fusion = f32[256,2048]{1,0:T(8,128)S(1)} fusion(bf16[2048,2048]{1,0:T(8,128)(2,1)} %all-gather.5.cloned.1.call-done, f32[1,256,2048]{2,1,0:T(8,128)} %param.15, bf16[256,2048]{1,0:T(8,128)(2,1)} %fusion.20, f32[2048]{0:T(1024)S(1)} %bitcast.118), kind=kOutput, calls=%fused_computation.39 | convolution fusion | flops 2149580800 | bytes 13639680 | tf_op jit(solution)/shard_map/dot_general | solution.py:30
  129.7 2.0 fusion.25
  132.2 23.4 %custom-call.8 = f32[1,8,32,32]{3,2,1,0:T(8,128)S(1)} custom-call(f32[1,8,32,32]{3,2,1,0:T(8,128)S(1)} %fusion.38), custom_call_target="Cholesky" | custom-call | tf_op jit(solution)/shard_map/jit(cholesky)/cholesky | solution.py:13
  155.9 19.7 %custom-call.9 = f32[8,1,32,32]{2,3,1,0:T(8,128)S(1)} custom-call(f32[8,1,32,32]{3,2,1,0:T(8,128)S(1)} %select_bitcast_fusion), custom_call_target="InvertDiagBlocksLowerTriangular" | custom-call | tf_op jit(solution)/shard_map/jit(_solve_triangular)/vmap()/triangular_solve | solution.py:14
  176.0 1.3 fusion.32
  178.1 2.2 reduce.17
  180.2 0.9 reshape.271
  181.1 10.0 %all-to-all-start = ((bf16[32,2,2048]{2,1,0:T(2,128)(2,1)}), bf16[32,2,2048]{2,1,0:T(2,128)(2,1)S(1)}, u32[]{:S(2)}, u32[]{:S(2)}) async-start(bf16[32,2,2048]{2,1,0:T(2,128)(2,1)} %reshape.271), calls=%async_computation | async-start | bytes 524288 | tf_op jit(solution)/shard_map/all_to_all | solution.py:81
  191.7 10.2 %all-to-all-done = bf16[32,2,2048]{2,1,0:T(2,128)(2,1)S(1)} async-done(((bf16[32,2,2048]{2,1,0:T(2,128)(2,1)}), bf16[32,2,2048]{2,1,0:T(2,128)(2,1)S(1)}, u32[]{:S(2)}, u32[]{:S(2)}) %all-to-all-start) | async-done | bytes 262176 | tf_op jit(solution)/shard_map/all_to_all | solution.py:81
  202.4 1.2 gather_fusion.2
  204.1 1.7 select_select_fusion
  205.8 6.5 %all-to-all-start.1 = ((bf16[32,4,4096]{2,1,0:T(4,128)(2,1)}), bf16[32,4,4096]{2,1,0:T(4,128)(2,1)S(1)}, u32[]{:S(2)}, u32[]{:S(2)}) async-start(bf16[32,4,4096]{2,1,0:T(4,128)(2,1)} %select_select_fusion), calls=%async_computation.1 | async-start | bytes 2097152 | tf_op jit(solution)/shard_map/all_to_all | solution.py:86
  212.7 24.9 %all-to-all-done.1 = bf16[32,4,4096]{2,1,0:T(4,128)(2,1)S(1)} async-done(((bf16[32,4,4096]{2,1,0:T(4,128)(2,1)}), bf16[32,4,4096]{2,1,0:T(4,128)(2,1)S(1)}, u32[]{:S(2)}, u32[]{:S(2)}) %all-to-all-start.1) | async-done | bytes 1048608 | tf_op jit(solution)/shard_map/all_to_all | solution.py:86
  238.7 4.3 broadcast_in_dim.118
  243.0 223.2 %while.18 = (s32[]{:T(128)}, f32[512,4096]{0,1:T(8,128)}, pred[4]{0:T(512)(128)(4,1)S(1)}, s32[4]{0:T(128)S(1)}, s32[]{:T(128)}, /*index=5*/s32[32,2048]{1,0:T(8...) while((s32[]{:T(128)}, f32[512,4096]{0,1:T(8,128)}, pred[4]{0:T(512)(128)(4,1)S(1)}, ...), condition=%wide.region_12.13_spmd.clone.clone, body=%wide.region_5.0_spmd.clone.clone.sunk | while | flops 48931344 | bytes 74002920 | solution.py:99
  244.2 54.5 %conditional.4 = (f32[512,4096]{0,1:T(8,128)}) conditional(s32[]{:T(128)} %bitcast.102, f32[512,4096]{0,1:T(8,128)} %get-tuple-element.358, (s32[]{:T(128)}, s32[4]{0:T(128)S(1)}, s32[]{:T(128)}, s32[32,2048]{1,0:T(8,128)}, s32[512]{0:T(512)S(1)}, /*index=5*/s32[512]{0:T(512)S(1)}, s32[256]{0:T(256)S(1)}, s32[8]{0:T(128)S(1)}, ...), branch_computations={%region_6.6_spmd, %region_7.11_spmd.clone} | conditional | flops 48931340 | bytes 73999632 | solution.py:92
  246.8 0.8 dynamic_slice.33
  247.8 1.8 fusion.9
  249.7 1.9 copy.75
  251.6 3.6 gather_fusion
  255.2 4.5 broadcast_select_fusion
  259.7 5.4 %copy.76 = f32[512,2048]{0,1:T(8,128)} copy(f32[512,2048]{1,0:T(8,128)} %broadcast_select_fusion) | data formatting | bytes 8388608 | tf_op jit(solution)/shard_map/while/body/eval_jaxpr/cond/branch_1_fun/jit(_take)/select_n | solution.py:65
  265.1 0.9 dynamic-slice_reduce_fusion
  266.8 20.2 %gather_fusion.1 = f32[4096,512]{1,0:T(8,128)} fusion(f32[512,2048]{0,1:T(8,128)} %copy.76, s32[4096]{0:T(1024)S(1)} %broadcast_clamp_fusion), kind=kCustom, calls=%fused_computation.1.clone | custom fusion | bytes 16793600 | tf_op jit(solution)/shard_map/while/body/eval_jaxpr/cond/branch_1_fun/jit(_take)/gather | solution.py:65
  287.3 0.7 compare_reduce_fusion
  288.0 10.8 %fusion.6 = f32[512,4096]{0,1:T(8,128)} fusion(f32[512,4096]{0,1:T(8,128)} %get-tuple-element.268, f32[4096,512]{1,0:T(8,128)} %gather_fusion.1, pred[4096]{0:T(1024)(128)(4,1)S(1)} %compare_and_fusion, pred[512]{0:T(512)(128)(4,1)S(1)} %compare_reduce_fusion.1, pred[4096]{0:T(1024)(128)(4,1)S(1)} %bitcast.113), kind=kLoop, calls=%fused_computation.7 | loop fusion | flops 8388608 | bytes 25174528 | tf_op jit(solution)/shard_map/while/body/eval_jaxpr/cond/branch_1_fun/add | solution.py:66
  300.0 54.5 %conditional.4 = (f32[512,4096]{0,1:T(8,128)}) conditional(s32[]{:T(128)} %bitcast.102, f32[512,4096]{0,1:T(8,128)} %get-tuple-element.358, (s32[]{:T(128)}, s32[4]{0:T(128)S(1)}, s32[]{:T(128)}, s32[32,2048]{1,0:T(8,128)}, s32[512]{0:T(512)S(1)}, /*index=5*/s32[512]{0:T(512)S(1)}, s32[256]{0:T(256)S(1)}, s32[8]{0:T(128)S(1)}, ...), branch_computations={%region_6.6_spmd, %region_7.11_spmd.clone} | conditional | flops 48931340 | bytes 73999632 | solution.py:92
  302.6 0.8 dynamic_slice.33
  303.6 1.8 fusion.9
  305.5 1.9 copy.75
  307.4 3.6 gather_fusion
  311.0 4.5 broadcast_select_fusion
  315.5 5.4 %copy.76 = f32[512,2048]{0,1:T(8,128)} copy(f32[512,2048]{1,0:T(8,128)} %broadcast_select_fusion) | data formatting | bytes 8388608 | tf_op jit(solution)/shard_map/while/body/eval_jaxpr/cond/branch_1_fun/jit(_take)/select_n | solution.py:65
  320.9 0.9 dynamic-slice_reduce_fusion
  322.6 20.2 %gather_fusion.1 = f32[4096,512]{1,0:T(8,128)} fusion(f32[512,2048]{0,1:T(8,128)} %copy.76, s32[4096]{0:T(1024)S(1)} %broadcast_clamp_fusion), kind=kCustom, calls=%fused_computation.1.clone | custom fusion | bytes 16793600 | tf_op jit(solution)/shard_map/while/body/eval_jaxpr/cond/branch_1_fun/jit(_take)/gather | solution.py:65
  343.1 0.7 compare_reduce_fusion
  343.8 10.8 %fusion.6 = f32[512,4096]{0,1:T(8,128)} fusion(f32[512,4096]{0,1:T(8,128)} %get-tuple-element.268, f32[4096,512]{1,0:T(8,128)} %gather_fusion.1, pred[4096]{0:T(1024)(128)(4,1)S(1)} %compare_and_fusion, pred[512]{0:T(512)(128)(4,1)S(1)} %compare_reduce_fusion.1, pred[4096]{0:T(1024)(128)(4,1)S(1)} %bitcast.113), kind=kLoop, calls=%fused_computation.7 | loop fusion | flops 8388608 | bytes 25174528 | tf_op jit(solution)/shard_map/while/body/eval_jaxpr/cond/branch_1_fun/add | solution.py:66
  355.8 54.5 %conditional.4 = (f32[512,4096]{0,1:T(8,128)}) conditional(s32[]{:T(128)} %bitcast.102, f32[512,4096]{0,1:T(8,128)} %get-tuple-element.358, (s32[]{:T(128)}, s32[4]{0:T(128)S(1)}, s32[]{:T(128)}, s32[32,2048]{1,0:T(8,128)}, s32[512]{0:T(512)S(1)}, /*index=5*/s32[512]{0:T(512)S(1)}, s32[256]{0:T(256)S(1)}, s32[8]{0:T(128)S(1)}, ...), branch_computations={%region_6.6_spmd, %region_7.11_spmd.clone} | conditional | flops 48931340 | bytes 73999632 | solution.py:92
  358.4 0.8 dynamic_slice.33
  359.4 1.8 fusion.9
  361.3 1.9 copy.75
  363.2 3.6 gather_fusion
  366.8 4.5 broadcast_select_fusion
  371.3 5.4 %copy.76 = f32[512,2048]{0,1:T(8,128)} copy(f32[512,2048]{1,0:T(8,128)} %broadcast_select_fusion) | data formatting | bytes 8388608 | tf_op jit(solution)/shard_map/while/body/eval_jaxpr/cond/branch_1_fun/jit(_take)/select_n | solution.py:65
  376.7 0.9 dynamic-slice_reduce_fusion
  378.4 20.2 %gather_fusion.1 = f32[4096,512]{1,0:T(8,128)} fusion(f32[512,2048]{0,1:T(8,128)} %copy.76, s32[4096]{0:T(1024)S(1)} %broadcast_clamp_fusion), kind=kCustom, calls=%fused_computation.1.clone | custom fusion | bytes 16793600 | tf_op jit(solution)/shard_map/while/body/eval_jaxpr/cond/branch_1_fun/jit(_take)/gather | solution.py:65
  398.9 0.7 compare_reduce_fusion
  399.6 10.8 %fusion.6 = f32[512,4096]{0,1:T(8,128)} fusion(f32[512,4096]{0,1:T(8,128)} %get-tuple-element.268, f32[4096,512]{1,0:T(8,128)} %gather_fusion.1, pred[4096]{0:T(1024)(128)(4,1)S(1)} %compare_and_fusion, pred[512]{0:T(512)(128)(4,1)S(1)} %compare_reduce_fusion.1, pred[4096]{0:T(1024)(128)(4,1)S(1)} %bitcast.113), kind=kLoop, calls=%fused_computation.7 | loop fusion | flops 8388608 | bytes 25174528 | tf_op jit(solution)/shard_map/while/body/eval_jaxpr/cond/branch_1_fun/add | solution.py:66
  411.6 54.5 %conditional.4 = (f32[512,4096]{0,1:T(8,128)}) conditional(s32[]{:T(128)} %bitcast.102, f32[512,4096]{0,1:T(8,128)} %get-tuple-element.358, (s32[]{:T(128)}, s32[4]{0:T(128)S(1)}, s32[]{:T(128)}, s32[32,2048]{1,0:T(8,128)}, s32[512]{0:T(512)S(1)}, /*index=5*/s32[512]{0:T(512)S(1)}, s32[256]{0:T(256)S(1)}, s32[8]{0:T(128)S(1)}, ...), branch_computations={%region_6.6_spmd, %region_7.11_spmd.clone} | conditional | flops 48931340 | bytes 73999632 | solution.py:92
  414.2 0.8 dynamic_slice.33
  415.2 1.8 fusion.9
  417.1 1.9 copy.75
  419.0 3.6 gather_fusion
  422.6 4.5 broadcast_select_fusion
  427.1 5.4 %copy.76 = f32[512,2048]{0,1:T(8,128)} copy(f32[512,2048]{1,0:T(8,128)} %broadcast_select_fusion) | data formatting | bytes 8388608 | tf_op jit(solution)/shard_map/while/body/eval_jaxpr/cond/branch_1_fun/jit(_take)/select_n | solution.py:65
  432.5 0.9 dynamic-slice_reduce_fusion
  434.2 20.2 %gather_fusion.1 = f32[4096,512]{1,0:T(8,128)} fusion(f32[512,2048]{0,1:T(8,128)} %copy.76, s32[4096]{0:T(1024)S(1)} %broadcast_clamp_fusion), kind=kCustom, calls=%fused_computation.1.clone | custom fusion | bytes 16793600 | tf_op jit(solution)/shard_map/while/body/eval_jaxpr/cond/branch_1_fun/jit(_take)/gather | solution.py:65
  454.7 0.7 compare_reduce_fusion
  455.4 10.8 %fusion.6 = f32[512,4096]{0,1:T(8,128)} fusion(f32[512,4096]{0,1:T(8,128)} %get-tuple-element.268, f32[4096,512]{1,0:T(8,128)} %gather_fusion.1, pred[4096]{0:T(1024)(128)(4,1)S(1)} %compare_and_fusion, pred[512]{0:T(512)(128)(4,1)S(1)} %compare_reduce_fusion.1, pred[4096]{0:T(1024)(128)(4,1)S(1)} %bitcast.113), kind=kLoop, calls=%fused_computation.7 | loop fusion | flops 8388608 | bytes 25174528 | tf_op jit(solution)/shard_map/while/body/eval_jaxpr/cond/branch_1_fun/add | solution.py:66
  466.2 8.9 %copy.72 = f32[512,4096]{1,0:T(8,128)} copy(f32[512,4096]{0,1:T(8,128)} %get-tuple-element.219) | data formatting | bytes 16777216 | tf_op jit(solution)/shard_map/while | solution.py:99
  475.1 8.1 %fusion.19 = bf16[1,512,4096]{2,1,0:T(8,128)(2,1)} fusion(f32[512,4096]{1,0:T(8,128)} %copy.72, bf16[1,512,4096]{2,1,0:T(8,128)(2,1)} %param.19), kind=kLoop, calls=%fused_computation.38 | loop fusion | flops 6291456 | bytes 16777216 | tf_op jit(solution)/shard_map/broadcast_in_dim | solution.py:101
  (126 shorter events, 16.1 us)
Async XLA Ops:
  6.5 57.1 %copy-start = (bf16[1,256,2048]{2,1,0:T(8,128)(2,1)S(1)}, bf16[1,256,2048]{2,1,0:T(8,128)(2,1)}, u32[]{:S(2)}) copy-start(bf16[1,256,2048]{2,1,0:T(8,128)(2,1)} %param.12) | copy-start | bytes 3145732
  6.5 57.1 %all-gather.3.cloned.1.call-start = ((), (), s32[]{:S(2)}) async-start(), calls=%async_computation.2 | async-start | bytes 9437184 | tf_op jit(solution)/shard_map/all_gather | solution.py:24
  7.3 63.2 %copy-start.3 = (s32[32]{0:T(128)S(1)}, s32[32]{0:T(128)}, u32[]{:S(2)}) copy-start(s32[32]{0:T(128)} %param.18) | copy-start | bytes 388
  7.3 115.7 %copy-start.4 = (f32[1,2048]{1,0:T(1,128)S(1)}, f32[1,2048]{1,0:T(1,128)}, u32[]{:S(2)}) copy-start(f32[1,2048]{1,0:T(1,128)} %param.14) | copy-start | bytes 24580
  7.3 115.7 %all-gather.5.cloned.1.call-start = ((), (), s32[]{:S(2)}) async-start(), calls=%async_computation.3 | async-start | bytes 9437184 | tf_op jit(solution)/shard_map/all_gather | solution.py:29
  123.0 6.7 %copy-start.2 = (f32[1,1,8,32,256]{4,3,2,1,0:T(8,128)S(1)}, f32[1,1,8,32,256]{4,3,2,1,0:T(8,128)}, u32[]{:S(2)}) copy-start(f32[1,1,8,32,256]{4,3,2,1,0:T(8,128)} %param.16) | copy-start | bytes 786436
  181.1 20.7 %all-to-all-start = ((bf16[32,2,2048]{2,1,0:T(2,128)(2,1)}), bf16[32,2,2048]{2,1,0:T(2,128)(2,1)S(1)}, u32[]{:S(2)}, u32[]{:S(2)}) async-start(bf16[32,2,2048]{2,1,0:T(2,128)(2,1)} %reshape.271), calls=%async_computation | async-start | bytes 524288 | tf_op jit(solution)/shard_map/all_to_all | solution.py:81
  205.8 31.8 %all-to-all-start.1 = ((bf16[32,4,4096]{2,1,0:T(4,128)(2,1)}), bf16[32,4,4096]{2,1,0:T(4,128)(2,1)S(1)}, u32[]{:S(2)}, u32[]{:S(2)}) async-start(bf16[32,4,4096]{2,1,0:T(4,128)(2,1)} %select_select_fusion), calls=%async_computation.1 | async-start | bytes 2097152 | tf_op jit(solution)/shard_map/all_to_all | solution.py:86
  475.1 8.1 %copy-start.1 = (bf16[1,256,2048]{2,1,0:T(8,128)(2,1)S(1)}, bf16[1,256,2048]{2,1,0:T(8,128)(2,1)}, u32[]{:S(2)}) copy-start(bf16[1,256,2048]{2,1,0:T(8,128)(2,1)} %param.12) | copy-start | bytes 3145732
Sparse Core Ops, SparseCore 0:
  9.2 54.4 all-gather.2
  70.5 52.4 all-gather.4
where the time goes:
time: 492 us; the launch traced here: 490 us
  local copies, waits for them, and re-layouts  155 us (32%)
  waiting for transfers between devices  144 us (29%)
  other arithmetic  125 us (25%)
  matrix products  24.7 us (5%)
  starting transfers between devices  16.5 us (3%)
  between operations  13.6 us (3%)
  loops' own time  10.9 us (2%)
    gather x8, local copies, waits for them, and re-layouts, place(): picked = jnp.take(jnp.take(dense, source_rows, axis=0), source_cols, axis=1)  95.3 us
    all_gather x1, waiting for transfers between devices, body(): lax.all_gather(pivot_inverse, 'panel', axis=1, tiled=True)[0]  56.4 us
    all_gather x1, waiting for transfers between devices, body(): gathered = lax.all_gather(factor, 'panel', axis=0, tiled=True)  52.2 us
    add x4, other arithmetic, place(): total + jnp.where(valid_rows[:, None] & valid_cols[None, :], picked, 0.0)  43 us
    all_to_all x1, waiting for transfers between devices, body(): lax.all_to_all(outgoing, 'front', split_axis=0, concat_axis=2, tiled=True)  24.9 us
    another operation x4, other arithmetic, compress_rows(): lower = jnp.linalg.cholesky(gram)  23.6 us
    select_n x4, local copies, waits for them, and re-layouts, place(): picked = jnp.take(jnp.take(dense, source_rows, axis=0), source_cols, axis=1)  21.4 us
    another operation x3, other arithmetic, compress_rows(): basis = jax.scipy.linalg.solve_triangular(lower, range_t, lower=True)  19.8 us
  transfers between devices with their start and end apart: 4, of which 4 were waited for; matrix products, arithmetic and copies ran while one was open for 0% of the time, Pallas kernels for 0%

commit v1 on v0

--- a/solution.py
+++ b/solution.py
@@ -26,7 +26,9 @@
     )
     factor = factor_sum.astype(jnp.bfloat16)
     scaled = (factor.astype(jnp.float32) / pivots[0][None, :]).astype(jnp.bfloat16)
-    gathered = lax.all_gather(factor, "panel", axis=0, tiled=True)
+    gathered = jnp.concatenate(
+        lax.all_to_all(jnp.stack([factor] * lax.axis_size("panel")), "panel", 0, 0), axis=0
+    )
     update = lax.dot_general(
         scaled, gathered, (((1,), (1,)), ((), ())), preferred_element_type=jnp.float32
     )

time: 492 us -> 542 us (1.10)
  waiting for transfers between devices: 144 us -> 186 us
    all_to_all x0 -> x1, waiting for transfers between devices: none -> 94.2 us  [body(): lax.all_to_all(jnp.stack([factor] * lax.axis_size('panel')), 'panel', 0, 0)]
    all_gather x1 -> x0, waiting for transfers between devices: 52.2 us -> none  [body(): gathered = lax.all_gather(factor, 'panel', axis=0, tiled=True)]
where the time goes in v1:
time: 542 us; the launch traced here: 540 us
  waiting for transfers between devices  186 us (34%)
  local copies, waits for them, and re-layouts  160 us (30%)
  other arithmetic  125 us (23%)
  matrix products  23.5 us (4%)
  starting transfers between devices  21.4 us (4%)
  between operations  13.6 us (3%)
  loops' own time  10.9 us (2%)
    gather x8, local copies, waits for them, and re-layouts, place(): picked = jnp.take(jnp.take(dense, source_rows, axis=0), source_cols, axis=1)  95.3 us
    all_to_all x1, waiting for transfers between devices, body(): lax.all_to_all(jnp.stack([factor] * lax.axis_size('panel')), 'panel', 0, 0)  94.2 us
    all_gather x1, waiting for transfers between devices, body(): lax.all_gather(pivot_inverse, 'panel', axis=1, tiled=True)[0]  56.4 us
    add x4, other arithmetic, place(): total + jnp.where(valid_rows[:, None] & valid_cols[None, :], picked, 0.0)  43 us
    all_to_all x1, waiting for transfers between devices, body(): lax.all_to_all(outgoing, 'front', split_axis=0, concat_axis=2, tiled=True)  24.7 us
    another operation x4, other arithmetic, compress_rows(): lower = jnp.linalg.cholesky(gram)  23.6 us
    select_n x4, local copies, waits for them, and re-layouts, place(): picked = jnp.take(jnp.take(dense, source_rows, axis=0), source_cols, axis=1)  21.4 us
    another operation x3, other arithmetic, compress_rows(): basis = jax.scipy.linalg.solve_triangular(lower, range_t, lower=True)  19.8 us
  transfers between devices with their start and end apart: 4, of which 4 were waited for; matrix products, arithmetic and copies ran while one was open for 0% of the time, Pallas kernels for 0%

profile of v1, /device:TPU:66, one launch (start us, length us, event | category | flops | bytes accessed | tf_op | source)
XLA Modules:
  0.0 540.2 jit_solution(18016392612269333732)
XLA Ops:
  7.3 56.4 %all-gather.2.cloned.1.call-done = bf16[1,2048,2048]{2,1,0:T(8,128)(2,1)} async-done(((bf16[1,256,2048]{2,1,0:T(8,128)(2,1)}), bf16[1,2048,2048]{2,1,0:T(8,128)(2,1)}) %all-gather.2.cloned.1.call-update) | async-done | bytes 8388624 | tf_op jit(solution)/shard_map/all_gather | solution.py:24
  63.7 5.7 %fusion.20 = bf16[256,2048]{1,0:T(8,128)(2,1)S(1)} fusion(bf16[1,2048,2048]{2,1,0:T(8,128)(2,1)} %all-gather.2.cloned.1.call-done, bf16[1,256,2048]{2,1,0:T(8,128)(2,1)S(1)} %copy-done), kind=kOutput, calls=%fused_computation.40 | convolution fusion | flops 2148007936 | bytes 10485760 | tf_op jit(solution)/shard_map/dot_general | solution.py:22
  69.4 1.0 copy-done.2
  70.4 4.3 stack.8
  74.6 5.1 all-to-all-start
  80.1 94.2 %all-to-all-done = bf16[8,256,2048]{2,1,0:T(8,128)(2,1)} async-done(((bf16[8,256,2048]{2,1,0:T(8,128)(2,1)}), bf16[8,256,2048]{2,1,0:T(8,128)(2,1)}, u32[]{:S(2)}, u32[]{:S(2)}) %all-to-all-start) | async-done | bytes 8388640 | tf_op jit(solution)/shard_map/all_to_all | solution.py:30
  174.3 6.4 %convolution_subtract_fusion = f32[256,2048]{1,0:T(8,128)S(1)} fusion(bf16[2048,2048]{1,0:T(8,128)(2,1)} %bitcast.16, f32[1,256,2048]{2,1,0:T(8,128)} %param.15, bf16[256,2048]{1,0:T(8,128)(2,1)S(1)} %copy-done.3, f32[2048]{0:T(1024)S(1)} %bitcast.119), kind=kOutput, calls=%fused_computation.39 | convolution fusion | flops 2149580800 | bytes 13639680 | tf_op jit(solution)/shard_map/dot_general | solution.py:32
  180.7 2.0 fusion.25
  183.3 23.4 %custom-call.8 = f32[1,8,32,32]{3,2,1,0:T(8,128)S(1)} custom-call(f32[1,8,32,32]{3,2,1,0:T(8,128)S(1)} %fusion.38), custom_call_target="Cholesky" | custom-call | tf_op jit(solution)/shard_map/jit(cholesky)/cholesky | solution.py:13
  207.0 19.7 %custom-call.9 = f32[8,1,32,32]{2,3,1,0:T(8,128)S(1)} custom-call(f32[8,1,32,32]{3,2,1,0:T(8,128)S(1)} %select_bitcast_fusion), custom_call_target="InvertDiagBlocksLowerTriangular" | custom-call | tf_op jit(solution)/shard_map/jit(_solve_triangular)/vmap()/triangular_solve | solution.py:14
  227.1 1.3 fusion.32
  229.1 2.2 reduce.17
  231.3 0.9 reshape.277
  232.2 10.0 %all-to-all-start.1 = ((bf16[32,2,2048]{2,1,0:T(2,128)(2,1)}), bf16[32,2,2048]{2,1,0:T(2,128)(2,1)S(1)}, u32[]{:S(2)}, u32[]{:S(2)}) async-start(bf16[32,2,2048]{2,1,0:T(2,128)(2,1)} %reshape.277), calls=%async_computation.1 | async-start | bytes 524288 | tf_op jit(solution)/shard_map/all_to_all | solution.py:83
  242.8 9.5 %all-to-all-done.1 = bf16[32,2,2048]{2,1,0:T(2,128)(2,1)S(1)} async-done(((bf16[32,2,2048]{2,1,0:T(2,128)(2,1)}), bf16[32,2,2048]{2,1,0:T(2,128)(2,1)S(1)}, u32[]{:S(2)}, u32[]{:S(2)}) %all-to-all-start.1) | async-done | bytes 262176 | tf_op jit(solution)/shard_map/all_to_all | solution.py:83
  252.9 1.2 gather_fusion.2
  254.5 1.7 select_select_fusion
  256.2 6.4 %all-to-all-start.2 = ((bf16[32,4,4096]{2,1,0:T(4,128)(2,1)}), bf16[32,4,4096]{2,1,0:T(4,128)(2,1)S(1)}, u32[]{:S(2)}, u32[]{:S(2)}) async-start(bf16[32,4,4096]{2,1,0:T(4,128)(2,1)} %select_select_fusion), calls=%async_computation.2 | async-start | bytes 2097152 | tf_op jit(solution)/shard_map/all_to_all | solution.py:88
  263.0 24.7 %all-to-all-done.2 = bf16[32,4,4096]{2,1,0:T(4,128)(2,1)S(1)} async-done(((bf16[32,4,4096]{2,1,0:T(4,128)(2,1)}), bf16[32,4,4096]{2,1,0:T(4,128)(2,1)S(1)}, u32[]{:S(2)}, u32[]{:S(2)}) %all-to-all-start.2) | async-done | bytes 1048608 | tf_op jit(solution)/shard_map/all_to_all | solution.py:88
  288.8 4.3 broadcast_in_dim.118
  293.1 223.2 %while.18 = (s32[]{:T(128)}, f32[512,4096]{0,1:T(8,128)}, pred[4]{0:T(512)(128)(4,1)S(1)}, s32[4]{0:T(128)S(1)}, s32[]{:T(128)}, /*index=5*/s32[32,2048]{1,0:T(8...) while((s32[]{:T(128)}, f32[512,4096]{0,1:T(8,128)}, pred[4]{0:T(512)(128)(4,1)S(1)}, ...), condition=%wide.region_12.13_spmd.clone.clone, body=%wide.region_5.0_spmd.clone.clone.sunk | while | flops 48931344 | bytes 74002920 | solution.py:101
  294.3 54.5 %conditional.4 = (f32[512,4096]{0,1:T(8,128)}) conditional(s32[]{:T(128)} %bitcast.103, f32[512,4096]{0,1:T(8,128)} %get-tuple-element.358, (s32[]{:T(128)}, s32[4]{0:T(128)S(1)}, s32[]{:T(128)}, s32[32,2048]{1,0:T(8,128)}, s32[512]{0:T(512)S(1)}, /*index=5*/s32[512]{0:T(512)S(1)}, s32[256]{0:T(256)S(1)}, s32[8]{0:T(128)S(1)}, ...), branch_computations={%region_6.6_spmd, %region_7.11_spmd.clone} | conditional | flops 48931340 | bytes 73999632 | solution.py:94
  296.9 0.8 dynamic_slice.33
  298.0 1.8 fusion.9
  299.8 1.9 copy.75
  301.7 3.6 gather_fusion
  305.3 4.5 broadcast_select_fusion
  309.8 5.4 copy.76
  315.2 0.9 dynamic-slice_reduce_fusion
  316.9 20.2 %gather_fusion.1 = f32[4096,512]{1,0:T(8,128)} fusion(f32[512,2048]{0,1:T(8,128)} %copy.76, s32[4096]{0:T(1024)S(1)} %broadcast_clamp_fusion), kind=kCustom, calls=%fused_computation.1.clone | custom fusion | bytes 16793600 | tf_op jit(solution)/shard_map/while/body/eval_jaxpr/cond/branch_1_fun/jit(_take)/gather | solution.py:67
  338.1 10.8 %fusion.6 = f32[512,4096]{0,1:T(8,128)} fusion(f32[512,4096]{0,1:T(8,128)} %get-tuple-element.268, f32[4096,512]{1,0:T(8,128)} %gather_fusion.1, pred[4096]{0:T(1024)(128)(4,1)S(1)} %compare_and_fusion, pred[512]{0:T(512)(128)(4,1)S(1)} %compare_reduce_fusion.1, pred[4096]{0:T(1024)(128)(4,1)S(1)} %bitcast.114), kind=kLoop, calls=%fused_computation.7 | loop fusion | flops 8388608 | bytes 25174528 | tf_op jit(solution)/shard_map/while/body/eval_jaxpr/cond/branch_1_fun/add | solution.py:68
  350.1 54.5 %conditional.4 = (f32[512,4096]{0,1:T(8,128)}) conditional(s32[]{:T(128)} %bitcast.103, f32[512,4096]{0,1:T(8,128)} %get-tuple-element.358, (s32[]{:T(128)}, s32[4]{0:T(128)S(1)}, s32[]{:T(128)}, s32[32,2048]{1,0:T(8,128)}, s32[512]{0:T(512)S(1)}, /*index=5*/s32[512]{0:T(512)S(1)}, s32[256]{0:T(256)S(1)}, s32[8]{0:T(128)S(1)}, ...), branch_computations={%region_6.6_spmd, %region_7.11_spmd.clone} | conditional | flops 48931340 | bytes 73999632 | solution.py:94
  352.7 0.8 dynamic_slice.33
  353.8 1.8 fusion.9
  355.6 1.9 copy.75
  357.5 3.6 gather_fusion
  361.1 4.5 broadcast_select_fusion
  365.6 5.4 copy.76
  371.0 0.9 dynamic-slice_reduce_fusion
  372.7 20.2 %gather_fusion.1 = f32[4096,512]{1,0:T(8,128)} fusion(f32[512,2048]{0,1:T(8,128)} %copy.76, s32[4096]{0:T(1024)S(1)} %broadcast_clamp_fusion), kind=kCustom, calls=%fused_computation.1.clone | custom fusion | bytes 16793600 | tf_op jit(solution)/shard_map/while/body/eval_jaxpr/cond/branch_1_fun/jit(_take)/gather | solution.py:67
  393.9 10.8 %fusion.6 = f32[512,4096]{0,1:T(8,128)} fusion(f32[512,4096]{0,1:T(8,128)} %get-tuple-element.268, f32[4096,512]{1,0:T(8,128)} %gather_fusion.1, pred[4096]{0:T(1024)(128)(4,1)S(1)} %compare_and_fusion, pred[512]{0:T(512)(128)(4,1)S(1)} %compare_reduce_fusion.1, pred[4096]{0:T(1024)(128)(4,1)S(1)} %bitcast.114), kind=kLoop, calls=%fused_computation.7 | loop fusion | flops 8388608 | bytes 25174528 | tf_op jit(solution)/shard_map/while/body/eval_jaxpr/cond/branch_1_fun/add | solution.py:68
  405.9 54.5 %conditional.4 = (f32[512,4096]{0,1:T(8,128)}) conditional(s32[]{:T(128)} %bitcast.103, f32[512,4096]{0,1:T(8,128)} %get-tuple-element.358, (s32[]{:T(128)}, s32[4]{0:T(128)S(1)}, s32[]{:T(128)}, s32[32,2048]{1,0:T(8,128)}, s32[512]{0:T(512)S(1)}, /*index=5*/s32[512]{0:T(512)S(1)}, s32[256]{0:T(256)S(1)}, s32[8]{0:T(128)S(1)}, ...), branch_computations={%region_6.6_spmd, %region_7.11_spmd.clone} | conditional | flops 48931340 | bytes 73999632 | solution.py:94
  408.5 0.8 dynamic_slice.33
  409.6 1.8 fusion.9
  411.4 1.9 copy.75
  413.3 3.6 gather_fusion
  416.9 4.5 broadcast_select_fusion
  421.4 5.4 copy.76
  426.8 0.9 dynamic-slice_reduce_fusion
  428.5 20.2 %gather_fusion.1 = f32[4096,512]{1,0:T(8,128)} fusion(f32[512,2048]{0,1:T(8,128)} %copy.76, s32[4096]{0:T(1024)S(1)} %broadcast_clamp_fusion), kind=kCustom, calls=%fused_computation.1.clone | custom fusion | bytes 16793600 | tf_op jit(solution)/shard_map/while/body/eval_jaxpr/cond/branch_1_fun/jit(_take)/gather | solution.py:67
  449.0 0.7 compare_reduce_fusion
  449.7 10.8 %fusion.6 = f32[512,4096]{0,1:T(8,128)} fusion(f32[512,4096]{0,1:T(8,128)} %get-tuple-element.268, f32[4096,512]{1,0:T(8,128)} %gather_fusion.1, pred[4096]{0:T(1024)(128)(4,1)S(1)} %compare_and_fusion, pred[512]{0:T(512)(128)(4,1)S(1)} %compare_reduce_fusion.1, pred[4096]{0:T(1024)(128)(4,1)S(1)} %bitcast.114), kind=kLoop, calls=%fused_computation.7 | loop fusion | flops 8388608 | bytes 25174528 | tf_op jit(solution)/shard_map/while/body/eval_jaxpr/cond/branch_1_fun/add | solution.py:68
  461.7 54.5 %conditional.4 = (f32[512,4096]{0,1:T(8,128)}) conditional(s32[]{:T(128)} %bitcast.103, f32[512,4096]{0,1:T(8,128)} %get-tuple-element.358, (s32[]{:T(128)}, s32[4]{0:T(128)S(1)}, s32[]{:T(128)}, s32[32,2048]{1,0:T(8,128)}, s32[512]{0:T(512)S(1)}, /*index=5*/s32[512]{0:T(512)S(1)}, s32[256]{0:T(256)S(1)}, s32[8]{0:T(128)S(1)}, ...), branch_computations={%region_6.6_spmd, %region_7.11_spmd.clone} | conditional | flops 48931340 | bytes 73999632 | solution.py:94
  464.3 0.8 dynamic_slice.33
  465.4 1.8 fusion.9
  467.2 1.9 copy.75
  469.1 3.6 gather_fusion
  472.7 4.5 broadcast_select_fusion
  477.2 5.4 copy.76
  482.6 0.9 dynamic-slice_reduce_fusion
  484.3 20.2 %gather_fusion.1 = f32[4096,512]{1,0:T(8,128)} fusion(f32[512,2048]{0,1:T(8,128)} %copy.76, s32[4096]{0:T(1024)S(1)} %broadcast_clamp_fusion), kind=kCustom, calls=%fused_computation.1.clone | custom fusion | bytes 16793600 | tf_op jit(solution)/shard_map/while/body/eval_jaxpr/cond/branch_1_fun/jit(_take)/gather | solution.py:67
  505.5 10.8 %fusion.6 = f32[512,4096]{0,1:T(8,128)} fusion(f32[512,4096]{0,1:T(8,128)} %get-tuple-element.268, f32[4096,512]{1,0:T(8,128)} %gather_fusion.1, pred[4096]{0:T(1024)(128)(4,1)S(1)} %compare_and_fusion, pred[512]{0:T(512)(128)(4,1)S(1)} %compare_reduce_fusion.1, pred[4096]{0:T(1024)(128)(4,1)S(1)} %bitcast.114), kind=kLoop, calls=%fused_computation.7 | loop fusion | flops 8388608 | bytes 25174528 | tf_op jit(solution)/shard_map/while/body/eval_jaxpr/cond/branch_1_fun/add | solution.py:68
  516.3 8.9 %copy.72 = f32[512,4096]{1,0:T(8,128)} copy(f32[512,4096]{0,1:T(8,128)} %get-tuple-element.219) | data formatting | bytes 16777216 | tf_op jit(solution)/shard_map/while | solution.py:101
  525.2 8.1 %fusion.19 = bf16[1,512,4096]{2,1,0:T(8,128)(2,1)} fusion(f32[512,4096]{1,0:T(8,128)} %copy.72, bf16[1,512,4096]{2,1,0:T(8,128)(2,1)} %param.19), kind=kLoop, calls=%fused_computation.38 | loop fusion | flops 6291456 | bytes 16777216 | tf_op jit(solution)/shard_map/broadcast_in_dim | solution.py:103
  (130 shorter events, 18.2 us)
Async XLA Ops:
  6.5 57.1 %copy-start = (bf16[1,256,2048]{2,1,0:T(8,128)(2,1)S(1)}, bf16[1,256,2048]{2,1,0:T(8,128)(2,1)}, u32[]{:S(2)}) copy-start(bf16[1,256,2048]{2,1,0:T(8,128)(2,1)} %param.12) | copy-start | bytes 3145732
  6.5 57.1 %all-gather.2.cloned.1.call-start = ((), (), s32[]{:S(2)}) async-start(), calls=%async_computation.3 | async-start | bytes 9437184 | tf_op jit(solution)/shard_map/all_gather | solution.py:24
  69.4 1.0 copy-start.2
  74.6 5.1 copy-start.5
  74.6 99.7 %copy-start.3 = (bf16[256,2048]{1,0:T(8,128)(2,1)S(1)}, bf16[256,2048]{1,0:T(8,128)(2,1)}, u32[]{:S(2)}) copy-start(bf16[256,2048]{1,0:T(8,128)(2,1)} %copy-done.2) | copy-start | bytes 3145732
  74.6 99.7 %copy-start.6 = (f32[1,2048]{1,0:T(1,128)S(1)}, f32[1,2048]{1,0:T(1,128)}, u32[]{:S(2)}) copy-start(f32[1,2048]{1,0:T(1,128)} %param.14) | copy-start | bytes 24580
  74.6 99.7 %all-to-all-start = ((bf16[8,256,2048]{2,1,0:T(8,128)(2,1)}), bf16[8,256,2048]{2,1,0:T(8,128)(2,1)}, u32[]{:S(2)}, u32[]{:S(2)}) async-start(bf16[8,256,2048]{2,1,0:T(8,128)(2,1)} %stack.8), calls=%async_computation | async-start | bytes 16777216 | tf_op jit(solution)/shard_map/all_to_all | solution.py:30
  174.3 6.4 %copy-start.4 = (f32[1,1,8,32,256]{4,3,2,1,0:T(8,128)S(1)}, f32[1,1,8,32,256]{4,3,2,1,0:T(8,128)}, u32[]{:S(2)}) copy-start(f32[1,1,8,32,256]{4,3,2,1,0:T(8,128)} %param.16) | copy-start | bytes 786436
  232.2 20.1 %all-to-all-start.1 = ((bf16[32,2,2048]{2,1,0:T(2,128)(2,1)}), bf16[32,2,2048]{2,1,0:T(2,128)(2,1)S(1)}, u32[]{:S(2)}, u32[]{:S(2)}) async-start(bf16[32,2,2048]{2,1,0:T(2,128)(2,1)} %reshape.277), calls=%async_computation.1 | async-start | bytes 524288 | tf_op jit(solution)/shard_map/all_to_all | solution.py:83
  256.2 31.5 %all-to-all-start.2 = ((bf16[32,4,4096]{2,1,0:T(4,128)(2,1)}), bf16[32,4,4096]{2,1,0:T(4,128)(2,1)S(1)}, u32[]{:S(2)}, u32[]{:S(2)}) async-start(bf16[32,4,4096]{2,1,0:T(4,128)(2,1)} %select_select_fusion), calls=%async_computation.2 | async-start | bytes 2097152 | tf_op jit(solution)/shard_map/all_to_all | solution.py:88
  525.2 8.1 %copy-start.1 = (bf16[1,256,2048]{2,1,0:T(8,128)(2,1)S(1)}, bf16[1,256,2048]{2,1,0:T(8,128)(2,1)}, u32[]{:S(2)}) copy-start(bf16[1,256,2048]{2,1,0:T(8,128)(2,1)} %param.12) | copy-start | bytes 3145732
Sparse Core Ops, SparseCore 0:
  9.2 54.4 all-gather.1
